TPU v7x, 32 devices: a whole 2x2x4 slice. The times are simulated.
32 devices in a mesh: bl: 8 (over z, x), tm: 4 (over y, core).
Axes of the slice: x: 2, y: 2, z: 4, core: 2. Of those that a mesh axis runs over, the one named last changes fastest.
Arguments:
- visibility_real: bfloat16 [3072, 16, 1024], P('bl', 'tm'), may hold values from -6 to 6
- visibility_imag: bfloat16 [3072, 16, 1024], P('bl', 'tm'), may hold values from -6 to 6
- weights: int32 [3072, 16], P('bl', 'tm'), may hold values from 0 to 8
- labels: int32 [3072], P('bl'), may hold values from 0 to 511, as said below
- owner_of: int32 [512], replicated, may hold values from 0 to 7, as said below
Outputs:
- bandpower: float32 [512, 1024], P(('bl', 'tm'))
Inputs may be any that keep to these rules, and one draw needn't show every extreme that they name: Of the rows of one device, at most 72 have labels of groups with one owner, and these carry at most 18 different labels; in every draw some owner gets exactly 72 such rows with exactly 18 labels from every device. `owner_of`: every owner owns exactly 64 groups.
All inputs are finite; a program needn't handle non-finite values.
Results may differ from a plain program's by a relative error of at most 0.0003.
Values may be sent and summed in bfloat16 or wider, within the bound.
A program may use at most 128 MiB of HBM per device.

v0:
```python
import functools
import math

import jax
import jax.numpy as jnp
from jax import lax
from jax.experimental import pallas as pl
from jax.experimental.pallas import tpu as pltpu
from jax.sharding import PartitionSpec as P

HARRIS = (0.35875, 0.48829, 0.14128, 0.01168)
RADIX = 4


def taper_of(length):
    phase_angle = 2.0 * math.pi / length * jnp.arange(length, dtype=jnp.float32)
    taper = (
        HARRIS[0]
        - HARRIS[1] * jnp.cos(phase_angle)
        + HARRIS[2] * jnp.cos(2.0 * phase_angle)
        - HARRIS[3] * jnp.cos(3.0 * phase_angle)
    )
    return taper / jnp.sqrt(jnp.sum(taper * taper))


def dft_table(channels):
    short = channels // RADIX
    fine = math.isqrt(short)
    turn = 2.0 * math.pi / channels
    delay = (
        RADIX * jnp.arange(short, dtype=jnp.int32)[None, None, :]
        + jnp.arange(RADIX, dtype=jnp.int32)[:, None, None]
    )

    def wave(rows):
        angle = turn * (rows[None, :, None] * delay % channels).astype(jnp.float32)
        return lax.optimization_barrier((jnp.cos(angle), jnp.sin(angle)))

    coarse_cos, coarse_sin = wave(fine * jnp.arange(short // fine, dtype=jnp.int32))
    fine_cos, fine_sin = wave(jnp.arange(fine, dtype=jnp.int32))
    ac, as_ = coarse_cos[:, :, None, :], coarse_sin[:, :, None, :]
    bc, bs = fine_cos[:, None], fine_sin[:, None]
    cosine = (ac * bc - as_ * bs).reshape(RADIX, short, short)
    sine = (as_ * bc + ac * bs).reshape(RADIX, short, short)
    top = jnp.concatenate([cosine, -sine], axis=2)
    bottom = jnp.concatenate([sine, cosine], axis=2)
    return jnp.concatenate([top, bottom], axis=1)


def owner_rank(owner_of, owners):
    hits = (owner_of[:, None] == jnp.arange(owners, dtype=jnp.int32)[None, :]).astype(jnp.int32)
    earlier = jnp.cumsum(hits, axis=0) - hits
    return jnp.sum(earlier * hits, axis=1)


def slots(labels, owner_of, owners, distinct):
    groups = owner_of.shape[0]
    per_owner = groups // owners
    group_rank = owner_rank(owner_of, owners)
    label_match = labels[:, None] == jnp.arange(groups, dtype=jnp.int32)[None, :]
    group_key = owner_of * per_owner + group_rank
    local_key = jnp.sum(jnp.where(label_match, group_key[None, :], 0), axis=1)
    key_match = local_key[:, None] == jnp.arange(groups, dtype=jnp.int32)[None, :]
    present = jnp.any(key_match, axis=0).astype(jnp.int32).reshape(owners, per_owner)
    order_within = jnp.cumsum(present, axis=1) - present
    slot_of_key = (jnp.arange(owners, dtype=jnp.int32)[:, None] * distinct + order_within).reshape(
        groups
    )
    row_slot = jnp.sum(jnp.where(key_match, slot_of_key[None, :], 0), axis=1)
    slot_hit = (
        order_within[:, :, None] == jnp.arange(distinct, dtype=jnp.int32)[None, None, :]
    ) & (present[:, :, None] > 0)
    slot_rank = jnp.sum(
        jnp.where(slot_hit, jnp.arange(per_owner, dtype=jnp.int32)[None, :, None], 0), axis=1
    )
    return row_slot, slot_rank


def greet(axis, size):
    me = lax.axis_index(axis)
    barrier = pltpu.get_barrier_semaphore()
    for hop in range(1, size):
        pl.semaphore_signal(
            barrier,
            inc=1,
            device_id={axis: lax.rem(me + hop, size)},
            device_id_type=pl.DeviceIdType.MESH,
        )
    pl.semaphore_wait(barrier, size - 1)
    return me


def exchange_kernel(size, data, note, data_out, note_out, held, kept, sends, arrivals, local):
    me = greet("bl", size)
    copies = []
    for which, (source, target) in enumerate(((note, note_out), (data, data_out))):
        for hop in range(1, size):
            peer = lax.rem(me + hop, size)
            copy = pltpu.make_async_remote_copy(
                src_ref=source.at[peer],
                dst_ref=target.at[me],
                send_sem=sends.at[which, hop - 1],
                recv_sem=arrivals.at[which, hop - 1],
                device_id={"bl": peer},
                device_id_type=pl.DeviceIdType.MESH,
            )
            copy.start()
            copies.append(copy)
    inward = [
        pltpu.make_async_copy(data.at[me], held, local.at[0]),
        pltpu.make_async_copy(note.at[me], kept, local.at[1]),
    ]
    outward = [
        pltpu.make_async_copy(held, data_out.at[me], local.at[0]),
        pltpu.make_async_copy(kept, note_out.at[me], local.at[1]),
    ]
    for copy in inward:
        copy.start()
    for copy in inward:
        copy.wait()
    for copy in outward:
        copy.start()
    for copy in outward:
        copy.wait()
    for copy in copies:
        copy.wait()


def exchange(data, note):
    size = data.shape[0]
    anywhere = pl.BlockSpec(memory_space=pl.ANY)
    return pl.pallas_call(
        functools.partial(exchange_kernel, size),
        out_shape=[
            jax.ShapeDtypeStruct(data.shape, data.dtype),
            jax.ShapeDtypeStruct(note.shape, note.dtype),
        ],
        in_specs=[anywhere, anywhere],
        out_specs=[anywhere, anywhere],
        scratch_shapes=[
            pltpu.VMEM(data.shape[1:], data.dtype),
            pltpu.VMEM(note.shape[1:], note.dtype),
            pltpu.SemaphoreType.DMA((2, size - 1)),
            pltpu.SemaphoreType.DMA((2, size - 1)),
            pltpu.SemaphoreType.DMA((2,)),
        ],
        compiler_params=pltpu.CompilerParams(collective_id=0, has_side_effects=True),
        cost_estimate=pl.CostEstimate(
            flops=0, bytes_accessed=32 * data.size, transcendentals=0
        ),
    )(data, note)


def tail_kernel(size, spectrum, out, following, share, came, sends, arrivals, step_sems):
    radix, times, groups, width = spectrum.shape
    short = width // 2
    rows = groups // size
    me = greet("tm", size)
    ahead = pltpu.make_async_remote_copy(
        src_ref=spectrum.at[:, 0],
        dst_ref=following,
        send_sem=step_sems.at[0],
        recv_sem=step_sems.at[1],
        device_id={"tm": lax.rem(me + size - 1, size)},
        device_id_type=pl.DeviceIdType.MESH,
    )
    ahead.start()
    for q in range(radix):
        pair = spectrum[q, 0] * spectrum[q, 1]
        for t in range(1, times - 1):
            pair += spectrum[q, t] * spectrum[q, t + 1]
        power = pair[:, :short] + pair[:, short:]
        for p in range(size):
            share[p, q] = power[p * rows : (p + 1) * rows]
    ahead.wait()
    for q in range(radix):
        pair = spectrum[q, times - 1] * following[q]
        power = pair[:, :short] + pair[:, short:]
        power = jnp.where(me < size - 1, power, 0.0)
        for p in range(size):
            share[p, q] += power[p * rows : (p + 1) * rows]
    copies = []
    for hop in range(1, size):
        peer = lax.rem(me + hop, size)
        copy = pltpu.make_async_remote_copy(
            src_ref=share.at[peer],
            dst_ref=came.at[hop - 1],
            send_sem=sends.at[hop - 1],
            recv_sem=arrivals.at[hop - 1],
            device_id={"tm": peer},
            device_id_type=pl.DeviceIdType.MESH,
        )
        copy.start()
        copies.append(copy)
    total = share[me]
    for hop, copy in enumerate(copies):
        copy.wait()
        total += came[hop]
    out[...] = total


def tail(spectrum, size):
    radix, times, groups, width = spectrum.shape
    block = (radix, groups // size, width // 2)
    inside = pl.BlockSpec(memory_space=pltpu.VMEM)
    return pl.pallas_call(
        functools.partial(tail_kernel, size),
        out_shape=jax.ShapeDtypeStruct(block, jnp.float32),
        in_specs=[inside],
        out_specs=inside,
        scratch_shapes=[
            pltpu.VMEM((radix, groups, width), jnp.float32),
            pltpu.VMEM((size,) + block, jnp.float32),
            pltpu.VMEM((size - 1,) + block, jnp.float32),
            pltpu.SemaphoreType.DMA((size - 1,)),
            pltpu.SemaphoreType.DMA((size - 1,)),
            pltpu.SemaphoreType.DMA((2,)),
        ],
        compiler_params=pltpu.CompilerParams(collective_id=1, has_side_effects=True),
    )(spectrum)


def per_device(visibility_real, visibility_imag, weights, labels, owner_of):
    row_count, times, channels = visibility_real.shape
    owners = lax.axis_size("bl")
    parts = lax.axis_size("tm")
    groups = owner_of.shape[0]
    per_owner = groups // owners
    capacity = 3 * row_count // (2 * owners)
    distinct = min(capacity // 4, per_owner // 2)
    row_slot, slot_rank = slots(labels, owner_of, owners, distinct)

    sent = distinct * times
    slot_id = jnp.arange(owners * sent, dtype=jnp.int32)[:, None]
    row_key = row_slot[:, None] * times + jnp.arange(times, dtype=jnp.int32)[None, :]
    row_key = row_key.reshape(1, row_count * times)
    row_weight = weights.astype(jnp.float32).reshape(1, row_count * times)
    folder = jnp.where(slot_id == row_key, row_weight, 0.0)
    part_weight = jnp.sum(folder, axis=1)
    folder = folder.astype(jnp.bfloat16)
    part_real = jnp.dot(
        folder,
        visibility_real.reshape(row_count * times, channels),
        preferred_element_type=jnp.float32,
    )
    part_imag = jnp.dot(
        folder,
        visibility_imag.reshape(row_count * times, channels),
        preferred_element_type=jnp.float32,
    )
    peak = jnp.maximum(
        jnp.max(jnp.abs(part_real), axis=1), jnp.max(jnp.abs(part_imag), axis=1)
    )
    step = lax.reduce_precision(jnp.maximum(peak, 1e-30) * (1.0078125 / 32767.0), 8, 7)
    invert = (1.0 / step)[:, None]
    code_real = jnp.round(part_real * invert).astype(jnp.int32)
    code_imag = jnp.round(part_imag * invert).astype(jnp.int32)
    packed = ((code_real << 16) | (code_imag & 65535)).reshape(owners, sent, channels)
    rank_row = jnp.broadcast_to(slot_rank[:, :, None], (owners, distinct, times))
    note = jnp.stack(
        [
            step.reshape(owners, sent),
            part_weight.reshape(owners, sent),
            rank_row.reshape(owners, sent).astype(jnp.float32),
        ],
        axis=1,
    )
    note = jnp.pad(note, ((0, 0), (0, 5), (0, -sent % 128)))
    came, came_note = exchange(packed, note)
    came_note = came_note[:, :, :sent]

    came_step = came_note[:, 0].reshape(1, owners * sent)
    came_weight = came_note[:, 1].reshape(1, owners * sent)
    came_rank = came_note[:, 2].reshape(1, owners * sent).astype(jnp.int32)
    came_time = jnp.arange(owners * sent, dtype=jnp.int32)[None, :] % times
    item = jnp.arange(times * per_owner, dtype=jnp.int32)[:, None]
    chosen = item == came_time * per_owner + came_rank
    selector = jnp.where(chosen, came_step, 0.0).astype(jnp.bfloat16)
    weight_sum = jnp.sum(jnp.where(chosen, came_weight, 0.0), axis=1)
    scale = (1.0 / jnp.maximum(weight_sum, 1.0)).reshape(times * per_owner, 1)

    came = came.reshape(owners * sent, channels)
    real_high = (came >> 24).astype(jnp.bfloat16)
    real_low = ((came >> 16) & 255).astype(jnp.bfloat16)
    imag_code = (came << 16) >> 16
    imag_high = (imag_code >> 8).astype(jnp.bfloat16)
    imag_low = (imag_code & 255).astype(jnp.bfloat16)

    def gather(high, low):
        upper = jnp.dot(selector, high, preferred_element_type=jnp.float32)
        lower = jnp.dot(selector, low, preferred_element_type=jnp.float32)
        return 256.0 * upper + lower

    taper = taper_of(channels)[None, :]
    mean_real = gather(real_high, real_low) * scale * taper
    mean_imag = gather(imag_high, imag_low) * scale * taper
    short = channels // RADIX
    r = [mean_real[:, i * short : (i + 1) * short] for i in range(RADIX)]
    m = [mean_imag[:, i * short : (i + 1) * short] for i in range(RADIX)]
    er, ei, fr, fi = r[0] + r[2], m[0] + m[2], r[1] + r[3], m[1] + m[3]
    gr, gi, hr, hi = r[0] - r[2], m[0] - m[2], r[1] - r[3], m[1] - m[3]
    folded = jnp.stack(
        [
            jnp.concatenate([er + fr, ei + fi], axis=1),
            jnp.concatenate([gr + hi, gi - hr], axis=1),
            jnp.concatenate([er - fr, ei - fi], axis=1),
            jnp.concatenate([gr - hi, gi + hr], axis=1),
        ]
    )
    spectrum = jnp.einsum(
        "qnf,qfk->qnk", folded, dft_table(channels), precision=lax.Precision.HIGH
    ).reshape(RADIX, times, per_owner, 2 * short)
    total = tail(spectrum, parts)
    return total.transpose(1, 2, 0).reshape(per_owner // parts, channels)


def solution(mesh):
    placed = (P("bl", "tm", None), P("bl", "tm", None), P("bl", "tm"), P("bl"), P())
    return jax.shard_map(
        per_device, mesh=mesh, in_specs=placed, out_specs=P(("bl", "tm"), None), check_vma=False
    )
```

profile of v0, /device:TPU:9, one launch (start us, length us, event | category | flops | bytes accessed | tf_op | source)
XLA Modules:
  0.0 120.5 jit_solution(5383760016451560581)
XLA Ops:
  0.0 0.7 fusion.64
  0.7 1.1 reduce-window.6
  1.8 0.2 slice_reduce_fusion
  2.1 0.8 fusion.63
  2.8 0.7 multiply_add_fusion.1
  3.5 0.9 select_reduce_fusion.2
  4.4 0.2 fusion.27
  4.6 0.1 reshape.276
  4.7 0.2 reduce_window_sum.30
  4.9 0.1 reduce_window_sum.31
  5.0 0.1 add.156
  5.1 0.1 add.157
  5.2 0.2 select_reduce_fusion.1
  5.4 0.1 iota_add_fusion
  5.6 0.1 add.162
  5.7 0.7 convert_element_type.109
  6.4 0.1 copy.10
  6.5 0.1 broadcast_in_dim.101
  6.7 5.5 %reshape.271 = bf16[1536,1024]{1,0:T(8,128)(2,1)} reshape(bf16[384,4,1024]{2,1,0:T(4,128)(2,1)} %param.5) | data formatting | bytes 6291456 | tf_op jit(solution)/shard_map/reshape | solution.py:243
  12.2 0.0 copy-start
  12.2 5.5 %abs_reduce_fusion.1 = (f32[576]{0:T(1024)S(1)}, f32[576,1024]{1,0:T(8,128)}) fusion(bf16[1536,1024]{1,0:T(8,128)(2,1)} %reshape.271, f32[1536]{0:T(1024)S(1)} %broadcast_in_dim.101, s32[1536]{0:T(1024)S(1)} %add.162), kind=kOutput, calls=%fused_computation.18 | convolution fusion | flops 1814887936 | bytes 5519616 | tf_op jit(solution)/shard_map/dot_general | solution.py:241
  17.7 0.0 copy-done
  17.7 3.0 %reshape.272 = bf16[1536,1024]{1,0:T(8,128)(2,1)} reshape(bf16[384,4,1024]{2,1,0:T(4,128)(2,1)S(1)} %copy-done) | data formatting | bytes 6291456 | tf_op jit(solution)/shard_map/reshape | solution.py:248
  20.7 0.0 copy-start.1
  20.7 4.1 %abs_reduce_fusion = (f32[576]{0:T(1024)S(1)}, f32[576,1024]{1,0:T(8,128)S(1)}) fusion(bf16[1536,1024]{1,0:T(8,128)(2,1)} %reshape.272, f32[1536]{0:T(1024)S(1)} %broadcast_in_dim.101, s32[1536]{0:T(1024)S(1)} %add.162), kind=kOutput, calls=%fused_computation.17 | convolution fusion | flops 1814887936 | bytes 5519616 | tf_op jit(solution)/shard_map/dot_general | solution.py:246
  24.8 0.0 copy-done.1
  24.8 1.9 %and_or_fusion = s32[576,1024]{1,0:T(8,128)} fusion(f32[576,1024]{1,0:T(8,128)S(1)} %get-tuple-element.42, f32[576,1024]{1,0:T(8,128)S(1)} %copy-done.1, f32[576]{0:T(1024)S(1)} %get-tuple-element.19), kind=kLoop, calls=%fused_computation.16 | loop fusion | flops 5308416 | bytes 7080192 | tf_op jit(solution)/shard_map/or | solution.py:258
  26.8 0.1 reduce_precision.18
  26.9 0.4 select_reduce_fusion.4
  27.3 0.1 copy.11
  27.3 0.5 select_reduce_fusion
  27.8 0.1 stack_reshape.4
  27.9 0.6 select_maximum_fusion.note
  28.5 54.5 %shard_map.55 = (s32[8,72,1024]{2,1,0:T(8,128)}, f32[8,8,128]{2,1,0:T(8,128)}) custom-call(s32[8,72,1024]{2,1,0:T(8,128)} %bitcast.35, f32[8,8,128]{2,1,0:T(8,128)} %select_maximum_fusion.note), custom_call_target="tpu_custom_call" | custom-call | bytes 18874368 | tf_op jit(solution)/shard_map/pallas_call | solution.py:132
  83.0 4.0 %and_convert_fusion = (bf16[8,72,1024]{2,1,0:T(8,128)(2,1)S(1)}, bf16[8,72,1024]{2,1,0:T(8,128)(2,1)}, bf16[8,72,1024]{2,1,0:T(8,128)(2,1)S(1)}, bf16[8,72,1024]{2,1,0:T(8,128)(2,1)S(1)}) fusion(s32[8,72,1024]{2,1,0:T(8,128)} %get-tuple-element.12), kind=kLoop, calls=%fused_computation.11 | loop fusion | flops 6488064 | bytes 7077888 | tf_op jit(solution)/shard_map/convert_element_type | solution.py:287
  87.0 0.8 convert_reduce_fusion
  87.8 0.1 convert_element_type.116
  87.9 0.9 slice_reduce_fusion.1
  88.7 0.1 broadcast_in_dim.107
  88.8 3.0 %convolution_multiply_fusion = f32[256,1024]{1,0:T(8,128)} fusion(bf16[576,1024]{1,0:T(8,128)(2,1)} %bitcast.42, bf16[576]{0:T(1024)(128)(2,1)S(1)} %broadcast_in_dim.107, s32[576]{0:T(1024)S(1)} %fusion.66), kind=kOutput, calls=%fused_computation.35 | convolution fusion | flops 302546944 | bytes 2231680 | tf_op jit(solution)/shard_map/dot_general | solution.py:290
  91.9 0.1 broadcast_in_dim.110
  91.9 0.2 select_reduce_fusion.3
  92.2 0.7 multiply_reduce_fusion
  93.6 0.1 fusion.79
  93.6 2.0 %fusion.26 = f32[256,1024]{1,0:T(8,128)S(1)} fusion(f32[256,1024]{1,0:T(8,128)} %convolution_multiply_fusion, bf16[576,1024]{1,0:T(8,128)(2,1)S(1)} %bitcast.37, f32[1024]{0:T(1024)S(1)} %fusion.79, f32[256]{0:T(256)S(1)} %maximum_divide_fusion, bf16[576]{0:T(1024)(128)(2,1)S(1)} %broadcast_in_dim.107, s32[576]{0:T(1024)S(1)} %fusion.66), kind=kOutput, calls=%fused_computation.41 | convolution fusion | flops 303071232 | bytes 3285376 | tf_op jit(solution)/shard_map/dot_general | solution.py:291
  95.6 0.1 fusion.47
  95.7 0.8 convolution_multiply_fusion.1
  96.5 0.8 fusion.24
  97.3 0.1 fusion.41
  97.4 0.1 maximum_bitcast_fusion
  97.5 0.1 fusion.43
  97.6 0.1 maximum_bitcast_fusion.1
  97.8 0.6 fusion.60
  98.3 0.3 multiply_add_fusion
  98.7 0.1 bitcast_negate_fusion
  98.7 3.6 %fusion = f32[4,256,512]{2,1,0:T(8,128)} fusion(f32[4,256,256]{2,1,0:T(8,128)S(1)} %bitcast.43, f32[4,256,256]{2,1,0:T(8,128)S(1)} %bitcast.38, f32[4,256,256]{2,1,0:T(8,128)S(1)} %bitcast_negate_fusion, f32[1,256,512]{2,1,0:T(8,128)S(1)} %get-tuple-element.44, f32[1,256,512]{2,1,0:T(8,128)S(1)} %get-tuple-element.46, ...), kind=kOutput, calls=%fused_computation.2 | convolution fusion | flops 1615331328 | bytes 7340032 | tf_op jit(solution)/shard_map/qnf,qfk->qnk/dot_general | solution.py:310
  102.4 16.2 %shard_map.56 = f32[4,16,256]{2,1,0:T(8,128)} custom-call(f32[4,4,64,512]{3,2,1,0:T(8,128)} %bitcast.40), custom_call_target="tpu_custom_call" | custom-call | tf_op jit(solution)/shard_map/pallas_call | solution.py:206
  118.6 1.1 copy.12
  119.7 0.8 copy.13
  (16 shorter events, 0.1 us)
Async XLA Ops:
  12.2 5.5 %copy-start = (bf16[384,4,1024]{2,1,0:T(4,128)(2,1)S(1)}, bf16[384,4,1024]{2,1,0:T(4,128)(2,1)}, u32[]{:S(2)}) copy-start(bf16[384,4,1024]{2,1,0:T(4,128)(2,1)} %param.6) | copy-start | bytes 9437188
  20.7 4.1 %copy-start.1 = (f32[576,1024]{1,0:T(8,128)S(1)}, f32[576,1024]{1,0:T(8,128)}, u32[]{:S(2)}) copy-start(f32[576,1024]{1,0:T(8,128)} %get-tuple-element.40) | copy-start | bytes 7077892
where the time goes:
time: 122 us; the launch traced here: 120 us
  Pallas kernels  70.7 us (58%)
  matrix products  19.8 us (16%)
  other arithmetic  16.3 us (13%)
  local copies, waits for them, and re-layouts  12.7 us (10%)
    pallas_call x1, Pallas kernels, exchange(): pl.pallas_call(functools.partial(exchange_kernel, size), out_shape=[jax.S...  54.5 us
    pallas_call x1, Pallas kernels, tail(): pl.pallas_call(functools.partial(tail_kernel, size), out_shape=jax.ShapeD...  16.2 us
    reshape x1, local copies, waits for them, and re-layouts, per_device(): visibility_real.reshape(row_count * times, channels)  5.53 us
    dot_general x1, matrix products, per_device(): jnp.dot(folder, visibility_real.reshape(row_count * times, channels), pre...  5.47 us
    dot_general x1, matrix products, per_device(): jnp.dot(folder, visibility_imag.reshape(row_count * times, channels), pre...  4.12 us
    convert_element_type x1, other arithmetic, per_device(): imag_low = (imag_code & 255).astype(jnp.bfloat16)  3.97 us
    dot_general x2, matrix products, gather(): upper = jnp.dot(selector, high, preferred_element_type=jnp.float32)  3.81 us
    dot_general x1, matrix products, per_device(): jnp.einsum('qnf,qfk->qnk', folded, dft_table(channels), precision=lax.Pre...  3.64 us

commit v1 on v0

v1 whole, which is shorter than its diff:
```python
import functools
import math

import jax
import jax.numpy as jnp
from jax import lax
from jax.experimental import pallas as pl
from jax.experimental.pallas import tpu as pltpu
from jax.sharding import PartitionSpec as P

HARRIS = (0.35875, 0.48829, 0.14128, 0.01168)
RADIX = 4
F32, BF16, I32 = jnp.float32, jnp.bfloat16, jnp.int32
MESH = pl.DeviceIdType.MESH


def iota(shape, dim):
    return lax.broadcasted_iota(I32, shape, dim)


def dot(a, b):
    return jnp.dot(a, b, preferred_element_type=F32)


def halves(value):
    high = value.astype(BF16)
    return high, (value - high.astype(F32)).astype(BF16)


def lanes(count):
    return -(-max(count, 1) // 128) * 128


def partner(me, step, size):
    if size & (size - 1):
        return lax.rem(me + step, size)
    peer, bit = 0, 1
    while bit < size:
        mine = lax.rem(me // bit, 2)
        peer = peer + bit * (1 - mine if step & bit else mine)
        bit *= 2
    return peer


class Plan:
    def __init__(self, row_count, times, channels, groups, owners, parts):
        capacity = 3 * row_count // (2 * owners)
        self.rows, self.times, self.channels, self.groups = row_count, times, channels, groups
        self.owners, self.parts = owners, parts
        self.per_owner = groups // owners
        self.distinct = min(capacity // 4, self.per_owner // 2)
        self.main = self.distinct // 8 * 8
        self.extra = self.distinct - self.main
        self.tail = -(-self.extra * times // 8) * 8
        self.mains = owners * self.main
        self.tails = owners * self.tail
        self.wide = max(lanes(self.mains), lanes(self.tails))
        self.facts = -(-(times + 4) // 8) * 8


def program_kernel(
    plan, vis_real, vis_imag, weights, labels, owner_of, out,
    fresh, part, part_tail, send, send_tail, send_note, send_step,
    came, came_tail, came_note, came_step,
    table, taper, total, spectrum, following, share, shared,
    loads, sends, arrivals, tail_sends, tail_arrivals,
):
    p = plan
    T, N, F, G, R = p.times, p.owners, p.channels, p.groups, p.rows
    pairs, both = T // 2, 2 * R
    short = F // RADIX
    me = lax.axis_index("bl")
    here = lax.axis_index("tm")

    incoming = []
    for pair in range(pairs):
        for which, source in enumerate((vis_real, vis_imag)):
            copy = pltpu.make_async_copy(
                source.at[:, pl.ds(2 * pair, 2)], fresh.at[pair, which], loads.at[pair, which]
            )
            copy.start()
            incoming.append(copy)

    barrier = pltpu.get_barrier_semaphore()
    for hop in range(1, N):
        pl.semaphore_signal(
            barrier, inc=1, device_id={"bl": lax.rem(me + hop, N)}, device_id_type=MESH
        )
    for hop in range(1, p.parts):
        pl.semaphore_signal(
            barrier, inc=1, device_id={"tm": lax.rem(here + hop, p.parts)}, device_id_type=MESH
        )

    label = labels[...]
    base = jnp.concatenate(
        [
            (label // 256).astype(F32),
            lax.rem(label, 256).astype(F32),
            weights[...].astype(F32),
            jnp.zeros((-(T + 2) % 8, R), F32),
        ],
        axis=0,
    )
    spread = (iota((R, both), 1) // 2 == iota((R, both), 0)).astype(F32).astype(BF16)
    doubled = dot(base.astype(BF16), spread)
    label_twice = (doubled[0:1] * 256.0 + doubled[1:2]).astype(I32)
    hit = (iota((G, both), 0) == label_twice).astype(F32).astype(BF16)
    count = lax.dot_general(
        jnp.ones((8, both), BF16), hit, (((1,), (1,)), ((), ())), preferred_element_type=F32
    )
    present = (count[0:1] > 0.5).astype(F32)
    owner = owner_of[...]
    owned = (iota((N, G), 0) == owner).astype(F32)
    before = (iota((G, G), 0) < iota((G, G), 1)).astype(F32).astype(BF16)
    earlier = dot(jnp.concatenate([owned, owned * present], axis=0).astype(BF16), before)
    rank = jnp.sum(owned * earlier[:N], axis=0, keepdims=True)
    order = jnp.sum(owned * earlier[N:], axis=0, keepdims=True)
    info = jnp.concatenate([owner.astype(F32), order, jnp.zeros((6, G), F32)], axis=0)
    placed = dot(info.astype(BF16), hit)
    row_owner = placed[0:1].astype(I32)
    row_order = placed[1:2].astype(I32)
    second = lax.rem(iota((1, both), 1), 2)

    listed = order.astype(I32)
    seen = present > 0.5
    rank_main = rank_tail = None
    if p.main:
        slot_main = jnp.where(seen & (listed < p.main), owner * p.main + listed, -1)
        rank_main = jnp.sum(
            jnp.where(iota((p.mains, G), 0) == slot_main, rank, 0.0), axis=1, keepdims=True
        )
    if p.extra:
        slot_tail = jnp.where(
            seen & (listed >= p.main), owner * p.extra + listed - p.main, -1
        )
        row = iota((p.tails, 1), 0)
        within = lax.rem(row, p.tail)
        slot_of_row = row // p.tail * p.extra + lax.rem(within, p.extra)
        rank_tail = jnp.sum(
            jnp.where((slot_of_row == slot_tail) & (within < p.extra * T), rank, 0.0),
            axis=1,
            keepdims=True,
        )

    def laid(column, height):
        block = jnp.broadcast_to(column, (column.shape[0], p.wide))
        shape = block.shape
        match = lax.rem(iota(shape, 0), height) == lax.rem(iota(shape, 1), height)
        block = jnp.where(match, block, 0.0).reshape(shape[0] // height, height, p.wide)
        return jnp.sum(block, axis=1, keepdims=True)

    send_note[...] = jnp.zeros_like(send_note)
    if p.main:
        send_note[:, 0:1] = laid(rank_main, p.main)
    if p.extra:
        send_note[:, T + 1 : T + 2] = laid(rank_tail, p.tail)

    def start(kind, peer):
        if kind < T:
            pieces = [(send.at[kind], came.at[kind], kind)]
            pieces.append((send_step.at[kind], came_step.at[kind], T + kind))
        else:
            pieces = [(send_note, came_note, 2 * T + 1)]
            if p.extra:
                pieces.append((send_tail, came_tail, 2 * T))
        return [
            pltpu.make_async_remote_copy(
                src_ref=source.at[peer],
                dst_ref=target.at[me],
                send_sem=sends.at[index, peer],
                recv_sem=arrivals.at[index, me],
                device_id={"bl": peer},
                device_id_type=MESH,
            )
            for source, target, index in pieces
        ]

    def arrive(kind, source):
        if kind < T:
            pieces = [(send.at[kind], came.at[kind], kind)]
            pieces.append((send_step.at[kind], came_step.at[kind], T + kind))
        else:
            pieces = [(send_note, came_note, 2 * T + 1)]
            if p.extra:
                pieces.append((send_tail, came_tail, 2 * T))
        return [
            pltpu.make_async_remote_copy(
                src_ref=origin.at[source],
                dst_ref=target.at[source],
                send_sem=sends.at[index, source],
                recv_sem=arrivals.at[index, source],
                device_id={"bl": source},
                device_id_type=MESH,
            )
            for origin, target, index in pieces
        ]

    def post(kind):
        for step in range(1, N):
            for copy in start(kind, partner(me, step, N)):
                copy.start()

    def encode(real, imag):
        peak = jnp.maximum(
            jnp.max(jnp.abs(real), axis=1, keepdims=True),
            jnp.max(jnp.abs(imag), axis=1, keepdims=True),
        )
        step = jnp.maximum(peak, 1e-30) * (1.0078125 / 32767.0)
        step = step.astype(BF16).astype(F32)
        invert = 1.0 / step
        code_real = jnp.round(real * invert).astype(I32)
        code_imag = jnp.round(imag * invert).astype(I32)
        return (code_real << 16) | (code_imag & 65535), step

    def encode_main(time):
        offset = time % 2 * p.mains

        def one(o, carry):
            at = pl.multiple_of(offset + o * p.main, 8)
            code, step = encode(part[0, pl.ds(at, p.main)], part[1, pl.ds(at, p.main)])
            send[time, o] = code
            send_step[time, o] = laid(step, p.main)[0]
            return carry

        lax.fori_loop(0, N, one, 0)
        came[time, me] = send[time, me]
        came_step[time, me] = send_step[time, me]

    def encode_tail():
        def one(o, carry):
            at = pl.multiple_of(o * p.tail, 8)
            code, step = encode(part_tail[0, pl.ds(at, p.tail)], part_tail[1, pl.ds(at, p.tail)])
            send_tail[o] = code
            send_note[o, T + 3 : T + 4] = laid(step, p.tail)[0]
            return carry

        lax.fori_loop(0, N, one, 0)
        came_tail[me] = send_tail[me]

    all_rows = 2 * p.mains + p.tails
    tail_weight = jnp.zeros((p.tails, 1), F32)
    for pair in range(pairs):
        weight = jnp.where(
            second == 0, doubled[2 + 2 * pair : 3 + 2 * pair], doubled[3 + 2 * pair : 4 + 2 * pair]
        )
        target = jnp.where(
            row_order < p.main,
            second * p.mains + row_owner * p.main + row_order,
            2 * p.mains
            + row_owner * p.tail
            + (2 * pair + second) * p.extra
            + row_order
            - p.main,
        )
        folder = jnp.where(iota((all_rows, both), 0) == target, weight, 0.0)
        sums = jnp.sum(folder, axis=1, keepdims=True)
        folder = folder.astype(BF16)
        for copy in incoming[2 * pair : 2 * pair + 2]:
            copy.wait()
        for which in range(2):
            made = dot(folder, fresh[pair, which].reshape(both, F))
            if p.main:
                part[which] = made[: 2 * p.mains]
            if p.extra:
                if pair:
                    part_tail[which] += made[2 * p.mains :]
                else:
                    part_tail[which] = made[2 * p.mains :]
        if p.main:
            send_note[:, 1 + 2 * pair : 2 + 2 * pair] = laid(sums[: p.mains], p.main)
            send_note[:, 2 + 2 * pair : 3 + 2 * pair] = laid(sums[p.mains : 2 * p.mains], p.main)
        if p.extra:
            tail_weight = tail_weight + sums[2 * p.mains :]
        if pair == 0:
            if p.main:
                encode_main(0)
            pl.semaphore_wait(barrier, N + p.parts - 2)
            if p.main:
                post(0)
                encode_main(1)
                if pairs == 1:
                    post(1)
        if pair == pairs - 1:
            if p.extra:
                send_note[:, T + 2 : T + 3] = laid(tail_weight, p.tail)
                encode_tail()
            came_note[me] = send_note[me]
            post(T)
            if p.main and pairs > 1:
                post(1)
        if p.main and pair:
            for time in (2 * pair, 2 * pair + 1):
                encode_main(time)
                post(time)

    turn = 2.0 * math.pi / F
    phase = turn * iota((1, F), 1).astype(F32)
    shape = (
        HARRIS[0]
        - HARRIS[1] * jnp.cos(phase)
        + HARRIS[2] * jnp.cos(2.0 * phase)
        - HARRIS[3] * jnp.cos(3.0 * phase)
    )
    taper[...] = shape / jnp.sqrt(jnp.sum(shape * shape, axis=1, keepdims=True))
    fine = 16
    for q in range(RADIX):
        delay = RADIX * iota((fine, short), 1) + q
        low = turn * lax.rem(iota((fine, short), 0) * delay, F).astype(F32)
        high = turn * lax.rem(fine * iota((fine, short), 0) * delay, F).astype(F32)
        low_cos, low_sin = jnp.cos(low), jnp.sin(low)
        high_cos, high_sin = jnp.cos(high), jnp.sin(high)
        for a in range(short // fine):
            ac, as_ = high_cos[a : a + 1], high_sin[a : a + 1]
            rows = pl.ds(a * fine, fine)
            upper, lower = halves(ac * low_cos - as_ * low_sin)
            table[q, 0, rows, :short] = upper
            table[q, 1, rows, :short] = lower
            upper, lower = halves(as_ * low_cos + ac * low_sin)
            table[q, 0, rows, short:] = upper
            table[q, 1, rows, short:] = lower

    def wait_for(kind):
        for step in range(1, N):
            for copy in arrive(kind, partner(me, step, N)):
                copy.wait_recv()

    def planes(code):
        real_high = (code >> 24).astype(F32).astype(BF16)
        real_low = ((code >> 16) & 255).astype(F32).astype(BF16)
        imag = (code << 16) >> 16
        imag_high = (imag >> 8).astype(F32).astype(BF16)
        imag_low = (imag & 255).astype(F32).astype(BF16)
        return (
            jnp.concatenate([real_high, real_low], axis=0),
            jnp.concatenate([imag_high, imag_low], axis=0),
        )

    def gathered(values, height):
        shape = values.shape
        mine = iota(shape, 2) // height == iota(shape, 0)
        return jnp.sum(jnp.where(mine, values, 0.0), axis=0)

    wait_for(T)
    facts = came_note[...]
    rank_row = iota((p.per_owner, 1), 0).astype(F32)
    chosen_main = facts_main = None
    if p.main:
        facts_main = gathered(facts, p.main)[:, : p.mains]
        chosen_main = rank_row == facts_main[0:1]
    tail_sums = []
    if p.extra:
        facts_tail = gathered(facts, p.tail)[:, : p.tails]
        tail_real, tail_imag = planes(came_tail[...].reshape(p.tails, F))
        lane = lax.rem(iota((1, p.tails), 1), p.tail)
        lane_time = jnp.where(lane < p.extra * T, lane // p.extra, T)
        selectors = []
        for time in range(T):
            chosen = (rank_row == facts_tail[T + 1 : T + 2]) & (lane_time == time)
            selector = jnp.where(chosen, facts_tail[T + 3 : T + 4], 0.0)
            selectors.append(jnp.concatenate([256.0 * selector, selector], axis=1))
            tail_sums.append(
                jnp.sum(
                    jnp.where(chosen, facts_tail[T + 2 : T + 3], 0.0), axis=1, keepdims=True
                )
            )
        selectors = jnp.concatenate(selectors, axis=0).astype(BF16)
        total[0] = dot(selectors, tail_real)
        total[1] = dot(selectors, tail_imag)
    for time in range(T):
        weight_sum = jnp.zeros((p.per_owner, 1), F32)
        if p.extra:
            weight_sum = weight_sum + tail_sums[time]
        block = pl.ds(time * p.per_owner, p.per_owner)
        real = imag = 0.0
        if p.extra:
            real, imag = total[0, block], total[1, block]
        if p.main:
            wait_for(time)
            steps = gathered(came_step[time], p.main)[:, : p.mains]
            selector = jnp.where(chosen_main, steps, 0.0)
            selector = jnp.concatenate([256.0 * selector, selector], axis=1).astype(BF16)
            weight_sum = weight_sum + jnp.sum(
                jnp.where(chosen_main, facts_main[1 + time : 2 + time], 0.0),
                axis=1,
                keepdims=True,
            )
            main_real, main_imag = planes(came[time].reshape(p.mains, F))
            real = real + dot(selector, main_real)
            imag = imag + dot(selector, main_imag)
        scale = 1.0 / jnp.maximum(weight_sum, 1.0)
        window = taper[...]
        real = real * scale * window
        imag = imag * scale * window
        r = [real[:, i * short : (i + 1) * short] for i in range(RADIX)]
        m = [imag[:, i * short : (i + 1) * short] for i in range(RADIX)]
        er, ei, fr, fi = r[0] + r[2], m[0] + m[2], r[1] + r[3], m[1] + m[3]
        gr, gi, hr, hi = r[0] - r[2], m[0] - m[2], r[1] - r[3], m[1] - m[3]
        folded = (
            (er + fr, ei + fi),
            (gr + hi, gi - hr),
            (er - fr, ei - fi),
            (gr - hi, gi + hr),
        )
        n = p.per_owner
        for q in range(RADIX):
            stacked = jnp.concatenate(folded[q], axis=0)
            upper, lower = halves(stacked)
            first = dot(jnp.concatenate([upper, lower], axis=0), table[q, 0])
            wave = first[: 2 * n] + first[2 * n :] + dot(upper, table[q, 1])
            spectrum[time, q, :, :short] = wave[:n, :short] + wave[n:, short:]
            spectrum[time, q, :, short:] = wave[n:, :short] - wave[:n, short:]
        if time == 0:
            ahead = pltpu.make_async_remote_copy(
                src_ref=spectrum.at[0],
                dst_ref=following,
                send_sem=tail_sends.at[p.parts - 1],
                recv_sem=tail_arrivals.at[p.parts - 1],
                device_id={"tm": lax.rem(here + p.parts - 1, p.parts)},
                device_id_type=MESH,
            )
            ahead.start()
        else:
            for q in range(RADIX):
                product = spectrum[time - 1, q] * spectrum[time, q]
                power = product[:, :short] + product[:, short:]
                power = power.reshape(p.parts, n // p.parts, short)
                if time == 1:
                    share[:, q] = power
                else:
                    share[:, q] += power
    ahead.wait()
    for q in range(RADIX):
        product = spectrum[T - 1, q] * following[q]
        power = product[:, :short] + product[:, short:]
        power = jnp.where(here < p.parts - 1, power, 0.0)
        share[:, q] += power.reshape(p.parts, p.per_owner // p.parts, short)
    copies = []
    for hop in range(1, p.parts):
        peer = lax.rem(here + hop, p.parts)
        copy = pltpu.make_async_remote_copy(
            src_ref=share.at[peer],
            dst_ref=shared.at[hop - 1],
            send_sem=tail_sends.at[hop - 1],
            recv_sem=tail_arrivals.at[hop - 1],
            device_id={"tm": peer},
            device_id_type=MESH,
        )
        copy.start()
        copies.append(copy)
    summed = share[here]
    for kind in range(T + 1):
        if kind == T or p.main:
            for step in range(1, N):
                for copy in start(kind, partner(me, step, N)):
                    copy.wait_send()
    for hop, copy in enumerate(copies):
        copy.wait()
        summed = summed + shared[hop]
    rows = p.per_owner // p.parts
    lane = iota((rows, 128), 1)
    for tile in range(F // 128):
        begin = tile * 128 // RADIX
        block = begin // 128 * 128
        index = lane // RADIX + (begin - block)
        value = None
        for q in range(RADIX):
            picked = jnp.take_along_axis(summed[q, :, block : block + 128], index, axis=1)
            value = picked if value is None else jnp.where(lax.rem(lane, RADIX) == q, picked, value)
        out[:, tile * 128 : (tile + 1) * 128] = value


def per_device(visibility_real, visibility_imag, weights, labels, owner_of):
    row_count, times, channels = visibility_real.shape
    owners, parts = lax.axis_size("bl"), lax.axis_size("tm")
    p = Plan(row_count, times, channels, owner_of.shape[0], owners, parts)
    short = channels // RADIX
    inside = pl.BlockSpec(memory_space=pltpu.VMEM)
    outside = pl.BlockSpec(memory_space=pltpu.HBM)
    some = lambda count: max(count, 8)
    main, tail = some(p.main), some(p.tail)
    rows = p.per_owner // parts
    return pl.pallas_call(
        functools.partial(program_kernel, p),
        out_shape=jax.ShapeDtypeStruct((rows, channels), F32),
        in_specs=[outside, outside, inside, inside, inside],
        out_specs=inside,
        scratch_shapes=[
            pltpu.VMEM((times // 2, 2, row_count, 2, channels), BF16),
            pltpu.VMEM((2, some(2 * p.mains), channels), F32),
            pltpu.VMEM((2, some(p.tails), channels), F32),
            pltpu.VMEM((times, owners, main, channels), I32),
            pltpu.VMEM((owners, tail, channels), I32),
            pltpu.VMEM((owners, p.facts, p.wide), F32),
            pltpu.VMEM((times, owners, 1, p.wide), F32),
            pltpu.VMEM((times, owners, main, channels), I32),
            pltpu.VMEM((owners, tail, channels), I32),
            pltpu.VMEM((owners, p.facts, p.wide), F32),
            pltpu.VMEM((times, owners, 1, p.wide), F32),
            pltpu.VMEM((RADIX, 2, short, 2 * short), BF16),
            pltpu.VMEM((1, channels), F32),
            pltpu.VMEM((2, times * p.per_owner, channels), F32),
            pltpu.VMEM((times, RADIX, p.per_owner, 2 * short), F32),
            pltpu.VMEM((RADIX, p.per_owner, 2 * short), F32),
            pltpu.VMEM((parts, RADIX, rows, short), F32),
            pltpu.VMEM((parts - 1, RADIX, rows, short), F32),
            pltpu.SemaphoreType.DMA((times // 2, 2)),
            pltpu.SemaphoreType.DMA((2 * times + 2, owners)),
            pltpu.SemaphoreType.DMA((2 * times + 2, owners)),
            pltpu.SemaphoreType.DMA((parts,)),
            pltpu.SemaphoreType.DMA((parts,)),
        ],
        compiler_params=pltpu.CompilerParams(
            collective_id=0, has_side_effects=True, vmem_limit_bytes=60 * 2**20
        ),
    )(visibility_real, visibility_imag, weights.T, labels[None, :], owner_of[None, :])


def solution(mesh):
    placed = (P("bl", "tm", None), P("bl", "tm", None), P("bl", "tm"), P("bl"), P())
    return jax.shard_map(
        per_device, mesh=mesh, in_specs=placed, out_specs=P(("bl", "tm"), None), check_vma=False
    )
```

time: 122 us -> 70.5 us (0.58); the launches traced: 120 us -> 70.3 us
  matrix products: 19.8 us -> 0 us
  other arithmetic: 16.3 us -> 0 us
  local copies, waits for them, and re-layouts: 12.7 us -> 2.72 us
  Pallas kernels: 70.7 us -> 67.5 us
    dot_general x7 -> x0, matrix products: 19.8 us -> none  [the longest x1 5.47 us: per_device(): jnp.dot(folder, visibility_real.reshape(row_count * times, channels), pre...]
    reshape x3 -> x0, local copies, waits for them, and re-layouts: 9.32 us -> none  [the longest x1 5.53 us: per_device(): visibility_real.reshape(row_count * times, channels)]
    convert_element_type x6 -> x0, other arithmetic: 6.14 us -> none  [the longest x1 3.97 us: per_device(): imag_low = (imag_code & 255).astype(jnp.bfloat16)]
    reduce_sum x7 -> x0, other arithmetic: 3.67 us -> none  [the longest x1 0.91 us: slots(): local_key = jnp.sum(jnp.where(label_match, group_key[None, :], 0), axis=1)]
    pallas_call x2 -> x1, Pallas kernels: 70.7 us -> 67.5 us  [per_device(): pl.pallas_call(functools.partial(program_kernel, p), out_shape=jax.ShapeD...]
    another operation x6 -> x0, other arithmetic: 2.26 us -> none
    or x1 -> x0, other arithmetic: 1.92 us -> none  [per_device(): code_real << 16 | code_imag & 65535]
    unnamed x4 -> x1, local copies, waits for them, and re-layouts: 0.01 us -> 1.47 us
where the time goes in v1:
time: 70.5 us; the launch traced here: 70.3 us
  Pallas kernels  67.5 us (96%)
  local copies, waits for them, and re-layouts  2.72 us (4%)
    pallas_call x1, Pallas kernels, per_device(): pl.pallas_call(functools.partial(program_kernel, p), out_shape=jax.ShapeD...  67.5 us
    unnamed x1, local copies, waits for them, and re-layouts  1.47 us

profile of v1, /device:TPU:9, one launch (start us, length us, event | category | flops | bytes accessed | tf_op | source)
XLA Modules:
  0.0 70.3 jit_solution(1812268169825381933)
XLA Ops:
  0.0 1.2 %broadcast_in_dim.6.labels = s32[1,384]{1,0:T(1,128)} reshape(s32[384]{0:T(512)} %param.8) | data formatting | bytes 3072 | tf_op jit(solution)/shard_map/broadcast_in_dim | solution.py:515
  1.2 67.5 %shard_map.55 = f32[16,1024]{1,0:T(8,128)} custom-call(bf16[384,4,1024]{2,1,0:T(4,128)(2,1)} %vis_real.1, bf16[384,4,1024]{2,1,0:T(4,128)(2,1)} %vis_imag.1, s32[4,384]{1,0:T(4,128)} %bitcast.2, s32[1,384]{1,0:T(1,128)} %broadcast_in_dim.6.labels, s32[1,512]{1,0:T(1,128)} %bitcast.3), custom_call_target="tpu_custom_call" | custom-call | tf_op jit(solution)/shard_map/pallas_call | solution.py:482
  68.8 1.5 %copy.7 = f32[16,1024]{1,0:T(8,128)} copy(f32[16,1024]{1,0:T(8,128)} %shard_map.55) | data formatting | bytes 131072

commit v2 on v1

v2 whole, which is shorter than its diff:
```python
import functools
import math

import jax
import jax.numpy as jnp
from jax import lax
from jax.experimental import pallas as pl
from jax.experimental.pallas import tpu as pltpu
from jax.sharding import PartitionSpec as P

HARRIS = (0.35875, 0.48829, 0.14128, 0.01168)
RADIX = 4
F32, BF16, I32 = jnp.float32, jnp.bfloat16, jnp.int32
MESH = pl.DeviceIdType.MESH


def iota(shape, dim):
    return lax.broadcasted_iota(I32, shape, dim)


def dot(a, b):
    return jnp.dot(a, b, preferred_element_type=F32)


def halves(value):
    high = value.astype(BF16)
    return high, (value - high.astype(F32)).astype(BF16)


def lanes(count):
    return -(-max(count, 1) // 128) * 128


def partner(me, step, size):
    if size & (size - 1):
        return lax.rem(me + step, size)
    peer, bit = 0, 1
    while bit < size:
        peer = peer + bit * lax.rem(lax.rem(me // bit, 2) + step // bit, 2)
        bit *= 2
    return peer


class Plan:
    def __init__(self, row_count, times, channels, groups, owners, parts):
        capacity = 3 * row_count // (2 * owners)
        self.rows, self.times, self.channels, self.groups = row_count, times, channels, groups
        self.owners, self.parts = owners, parts
        self.per_owner = groups // owners
        self.distinct = min(capacity // 4, self.per_owner // 2)
        self.main = self.distinct // 16 * 16
        self.extra = self.distinct - self.main
        self.tail = -(-self.extra * times // 8) * 8
        self.mains = owners * self.main
        self.tails = owners * self.tail
        assert times * self.main + 2 * self.tail <= 128


def program_kernel(
    plan, vis_real, vis_imag, weights, labels, owner_of, out,
    weight_in, label_in, owner_in,
    fresh, part, part_tail, send, send_tail, send_note, send_step,
    came, came_tail, came_note, came_step,
    table, taper, total, planes, spectrum, following, share, shared,
    loads, small, sends, arrivals, ahead_sems, tail_sends, tail_arrivals,
):
    p = plan
    T, N, F, G, R = p.times, p.owners, p.channels, p.groups, p.rows
    pairs, both = T // 2, 2 * R
    short = F // RADIX
    n = p.per_owner
    me = lax.axis_index("bl")
    here = lax.axis_index("tm")

    inputs = [
        pltpu.make_async_copy(source, target, small.at[index])
        for index, (source, target) in enumerate(
            ((labels, label_in), (weights, weight_in), (owner_of, owner_in))
        )
    ]
    for copy in inputs:
        copy.start()
    incoming = []
    for pair in range(pairs):
        for which, source in enumerate((vis_real, vis_imag)):
            copy = pltpu.make_async_copy(
                source.at[:, pl.ds(2 * pair, 2)], fresh.at[pair, which], loads.at[pair, which]
            )
            copy.start()
            incoming.append(copy)

    barrier = pltpu.get_barrier_semaphore()
    for hop in range(1, N):
        pl.semaphore_signal(
            barrier, inc=1, device_id={"bl": lax.rem(me + hop, N)}, device_id_type=MESH
        )
    for hop in range(1, p.parts):
        pl.semaphore_signal(
            barrier, inc=1, device_id={"tm": lax.rem(here + hop, p.parts)}, device_id_type=MESH
        )

    spread = (iota((R, both), 1) // 2 == iota((R, both), 0)).astype(F32).astype(BF16)
    before = (iota((G, G), 0) < iota((G, G), 1)).astype(F32).astype(BF16)
    for copy in inputs:
        copy.wait()
    label = jnp.concatenate(
        [label_in[i : i + 1] for i in range(label_in.shape[0])], axis=1
    )
    base = jnp.concatenate(
        [
            (label // 256).astype(F32),
            lax.rem(label, 256).astype(F32),
            weight_in[...].astype(F32),
            jnp.zeros((-(T + 2) % 8, R), F32),
        ],
        axis=0,
    )
    doubled = dot(base.astype(BF16), spread)
    label_twice = (doubled[0:1] * 256.0 + doubled[1:2]).astype(I32)
    hit = (iota((G, both), 0) == label_twice).astype(F32).astype(BF16)
    count = lax.dot_general(
        jnp.ones((8, both), BF16), hit, (((1,), (1,)), ((), ())), preferred_element_type=F32
    )
    present = (count[0:1] > 0.5).astype(F32)
    owner = owner_in[...]
    owned = (iota((N, G), 0) == owner).astype(F32)
    earlier = dot(jnp.concatenate([owned, owned * present], axis=0).astype(BF16), before)
    rank = jnp.sum(owned * earlier[:N], axis=0, keepdims=True)
    order = jnp.sum(owned * earlier[N:], axis=0, keepdims=True)
    info = jnp.concatenate([owner.astype(F32), order, jnp.zeros((6, G), F32)], axis=0)
    placed = dot(info.astype(BF16), hit)
    row_owner = placed[0:1].astype(I32)
    row_order = placed[1:2].astype(I32)
    second = lax.rem(iota((1, both), 1), 2)

    listed = order.astype(I32)
    seen = present > 0.5
    rank_main = rank_tail = None
    if p.main:
        slot_main = jnp.where(seen & (listed < p.main), owner * p.main + listed, -1)
        rank_main = jnp.sum(
            jnp.where(iota((p.mains, G), 0) == slot_main, rank, 0.0), axis=1, keepdims=True
        )
    if p.extra:
        slot_tail = jnp.where(
            seen & (listed >= p.main), owner * p.extra + listed - p.main, -1
        )
        row = iota((p.tails, 1), 0)
        within = lax.rem(row, p.tail)
        slot_of_row = row // p.tail * p.extra + lax.rem(within, p.extra)
        rank_tail = jnp.sum(
            jnp.where((slot_of_row == slot_tail) & (within < p.extra * T), rank, 0.0),
            axis=1,
            keepdims=True,
        )

    def laid(column, height, offset):
        shape = (column.shape[0], 128)
        match = lax.rem(iota(shape, 0), height) == iota(shape, 1) - offset
        block = jnp.where(match, jnp.broadcast_to(column, shape), 0.0)
        return jnp.sum(block.reshape(shape[0] // height, height, 128), axis=1, keepdims=True)

    base_tail = T * p.main
    note = jnp.zeros((N, 1, 128), F32)

    def start(kind, peer):
        if kind < T:
            pieces = [(send.at[kind], came.at[kind], kind)]
            pieces.append((send_step.at[kind], came_step.at[kind], T + kind))
        else:
            pieces = [(send_note, came_note, 2 * T + 1)]
            if p.extra:
                pieces.append((send_tail, came_tail, 2 * T))
        return [
            pltpu.make_async_remote_copy(
                src_ref=source.at[peer],
                dst_ref=target.at[me],
                send_sem=sends.at[index, peer],
                recv_sem=arrivals.at[index, me],
                device_id={"bl": peer},
                device_id_type=MESH,
            )
            for source, target, index in pieces
        ]

    def arrive(kind, source):
        if kind < T:
            pieces = [(send.at[kind], came.at[kind], kind)]
            pieces.append((send_step.at[kind], came_step.at[kind], T + kind))
        else:
            pieces = [(send_note, came_note, 2 * T + 1)]
            if p.extra:
                pieces.append((send_tail, came_tail, 2 * T))
        return [
            pltpu.make_async_remote_copy(
                src_ref=origin.at[source],
                dst_ref=target.at[source],
                send_sem=sends.at[index, source],
                recv_sem=arrivals.at[index, source],
                device_id={"bl": source},
                device_id_type=MESH,
            )
            for origin, target, index in pieces
        ]

    def post(kind, peer):
        for copy in start(kind, peer):
            copy.start()

    def encode(real, imag):
        peak = jnp.maximum(
            jnp.max(jnp.abs(real), axis=1, keepdims=True),
            jnp.max(jnp.abs(imag), axis=1, keepdims=True),
        )
        step = jnp.maximum(peak, 1e-30) * (1.0078125 / 32767.0)
        step = step.astype(BF16).astype(F32)
        invert = 1.0 / step
        code_real = jnp.round(real * invert).astype(I32)
        code_imag = jnp.round(imag * invert).astype(I32)
        return (code_real << 16) | (code_imag & 65535), step

    def encode_main(time, o):
        at = pl.multiple_of(time % 2 * p.mains + o * p.main, 16)
        rows = pl.ds(at, p.main)
        code, step = encode(part[time // 2, 0, rows], part[time // 2, 1, rows])
        return code, laid(step, p.main, 0)[0]

    def handle_main(time):
        def one(step, carry):
            peer = partner(me, step, N)
            code, steps = encode_main(time, peer)
            send[time, peer] = code
            send_step[time, peer] = steps
            post(time, peer)
            return carry

        lax.fori_loop(1, N, one, 0)
        code, steps = encode_main(time, me)
        came[time, me] = code
        came_step[time, me] = steps

    def encode_tail(o):
        at = pl.multiple_of(o * p.tail, 8)
        code, step = encode(part_tail[0, pl.ds(at, p.tail)], part_tail[1, pl.ds(at, p.tail)])
        return code, send_note[o] + laid(step, p.tail, base_tail + p.tail)[0]

    def handle_tail():
        def one(step, carry):
            peer = partner(me, step, N)
            if p.extra:
                code, facts = encode_tail(peer)
                send_tail[peer] = code
                send_note[peer] = facts
            post(T, peer)
            return carry

        lax.fori_loop(1, N, one, 0)
        if p.extra:
            code, facts = encode_tail(me)
            came_tail[me] = code
            came_note[me] = facts
        else:
            came_note[me] = send_note[me]

    all_rows = 2 * p.mains + p.tails
    tail_weight = jnp.zeros((p.tails, 1), F32)
    for pair in range(pairs):
        weight = jnp.where(
            second == 0, doubled[2 + 2 * pair : 3 + 2 * pair], doubled[3 + 2 * pair : 4 + 2 * pair]
        )
        target = jnp.where(
            row_order < p.main,
            second * p.mains + row_owner * p.main + row_order,
            2 * p.mains
            + row_owner * p.tail
            + (2 * pair + second) * p.extra
            + row_order
            - p.main,
        )
        folder = jnp.where(iota((all_rows, both), 0) == target, weight, 0.0)
        sums = jnp.sum(folder, axis=1, keepdims=True)
        folder = folder.astype(BF16)
        for copy in incoming[2 * pair : 2 * pair + 2]:
            copy.wait()
        for which in range(2):
            made = dot(folder, fresh[pair, which].reshape(both, F))
            if p.main:
                part[pair, which] = made[: 2 * p.mains]
            if p.extra:
                if pair:
                    part_tail[which] += made[2 * p.mains :]
                else:
                    part_tail[which] = made[2 * p.mains :]
        if p.main:
            for which in range(2):
                fact = sums[which * p.mains : (which + 1) * p.mains] * n + rank_main
                note = note + laid(fact, p.main, (2 * pair + which) * p.main)
        if p.extra:
            tail_weight = tail_weight + sums[2 * p.mains :]
        if pair == 0:
            pl.semaphore_wait(barrier, N + p.parts - 2)
            if p.main:
                handle_main(0)
        if pair == pairs - 1:
            if p.extra:
                note = note + laid(tail_weight * n + rank_tail, p.tail, base_tail)
            send_note[...] = note
            handle_tail()
            if p.main:
                handle_main(1)
        if p.main and pair:
            handle_main(2 * pair)
            handle_main(2 * pair + 1)

    turn = 2.0 * math.pi / F
    phase = turn * iota((1, F), 1).astype(F32)
    shape = (
        HARRIS[0]
        - HARRIS[1] * jnp.cos(phase)
        + HARRIS[2] * jnp.cos(2.0 * phase)
        - HARRIS[3] * jnp.cos(3.0 * phase)
    )
    taper[...] = shape / jnp.sqrt(jnp.sum(shape * shape, axis=1, keepdims=True))
    fine = 16
    for q in range(RADIX):
        delay = RADIX * iota((fine, short), 1) + q
        low = turn * lax.rem(iota((fine, short), 0) * delay, F).astype(F32)
        high = turn * lax.rem(fine * iota((fine, short), 0) * delay, F).astype(F32)
        low_cos, low_sin = jnp.cos(low), jnp.sin(low)
        high_cos, high_sin = jnp.cos(high), jnp.sin(high)
        for a in range(short // fine):
            ac, as_ = high_cos[a : a + 1], high_sin[a : a + 1]
            rows = pl.ds(a * fine, fine)
            upper, lower = halves(ac * low_cos - as_ * low_sin)
            table[q, 0, rows, :short] = upper
            table[q, 1, rows, :short] = lower
            upper, lower = halves(as_ * low_cos + ac * low_sin)
            table[q, 0, rows, short:] = upper
            table[q, 1, rows, short:] = lower

    def wait_for(kind, source):
        for copy in arrive(kind, source):
            copy.wait_recv()

    def split(code):
        imag = (code << 16) >> 16
        parts = (code >> 24, (code >> 16) & 255, imag >> 8, imag & 255)
        return [part.astype(F32).astype(BF16) for part in parts]

    def gathered(values, height, offset):
        values = values.reshape(N, 128)
        blocks = []
        for block in range(lanes(N * height) // 128):
            lane = iota((N, 128), 1) + block * 128
            picked = jnp.take_along_axis(values, offset + lax.rem(lane, height), axis=1)
            mine = lane // height == iota((N, 128), 0)
            blocks.append(jnp.sum(jnp.where(mine, picked, 0.0), axis=0, keepdims=True))
        return jnp.concatenate(blocks, axis=1)[:, : N * height]

    def facts_of(values, height, offset):
        fact = gathered(values, height, offset).astype(I32)
        return lax.rem(fact, n), (fact // n).astype(F32)

    for step in range(1, N):
        wait_for(T, partner(me, step, N))
    notes = came_note[...]
    rank_row = iota((n, 1), 0)
    main_facts = []
    if p.main:
        main_facts = [facts_of(notes, p.main, time * p.main) for time in range(T)]
    tail_sums = []
    if p.extra:
        tail_rank, tail_heft = facts_of(notes, p.tail, base_tail)
        tail_step = gathered(notes, p.tail, base_tail + p.tail)
        pieces = split(came_tail[...].reshape(p.tails, F))
        lane = lax.rem(iota((1, p.tails), 1), p.tail)
        lane_time = jnp.where(lane < p.extra * T, lane // p.extra, T)
        selectors = []
        for time in range(T):
            chosen = (rank_row == tail_rank) & (lane_time == time)
            selector = jnp.where(chosen, tail_step, 0.0)
            selectors.append(jnp.concatenate([256.0 * selector, selector], axis=1))
            tail_sums.append(jnp.sum(jnp.where(chosen, tail_heft, 0.0), axis=1, keepdims=True))
        selectors = jnp.concatenate(selectors, axis=0).astype(BF16)
        total[0] = dot(selectors, jnp.concatenate(pieces[:2], axis=0))
        total[1] = dot(selectors, jnp.concatenate(pieces[2:], axis=0))

    ahead = pltpu.make_async_remote_copy(
        src_ref=spectrum.at[0],
        dst_ref=following,
        send_sem=ahead_sems.at[0],
        recv_sem=ahead_sems.at[1],
        device_id={"tm": lax.rem(here + p.parts - 1, p.parts)},
        device_id_type=MESH,
    )
    rows = n // p.parts

    def across(hop, q):
        return pltpu.make_async_remote_copy(
            src_ref=share.at[lax.rem(here + hop, p.parts), q],
            dst_ref=shared.at[hop - 1, q],
            send_sem=tail_sends.at[hop - 1, q],
            recv_sem=tail_arrivals.at[hop - 1, q],
            device_id={"tm": lax.rem(here + hop, p.parts)},
            device_id_type=MESH,
        )

    def power_of(product):
        return (product[:, :short] + product[:, short:]).reshape(p.parts, rows, short)

    for time in range(T):
        weight_sum = jnp.zeros((n, 1), F32)
        if p.extra:
            weight_sum = weight_sum + tail_sums[time]
        if p.main:

            def unpack(source):
                for which, piece in enumerate(split(came[time, source])):
                    at = which % 2 * p.mains + source * p.main
                    planes[which // 2, pl.ds(pl.multiple_of(at, 16), p.main)] = piece

            def one(step, carry):
                source = partner(me, step, N)
                wait_for(time, source)
                unpack(source)
                return carry

            unpack(me)
            lax.fori_loop(1, N, one, 0)
            rank, heft = main_facts[time]
            chosen = rank_row == rank
            selector = jnp.where(chosen, gathered(came_step[time], p.main, 0), 0.0)
            selector = jnp.concatenate([256.0 * selector, selector], axis=1).astype(BF16)
            weight_sum = weight_sum + jnp.sum(jnp.where(chosen, heft, 0.0), axis=1, keepdims=True)
            real, imag = dot(selector, planes[0]), dot(selector, planes[1])
        block = pl.ds(time * n, n)
        if p.main and p.extra:
            real, imag = real + total[0, block], imag + total[1, block]
        elif p.extra:
            real, imag = total[0, block], total[1, block]
        scale = 1.0 / jnp.maximum(weight_sum, 1.0)
        window = taper[...]
        real = real * scale * window
        imag = imag * scale * window
        r = [real[:, i * short : (i + 1) * short] for i in range(RADIX)]
        m = [imag[:, i * short : (i + 1) * short] for i in range(RADIX)]
        er, ei, fr, fi = r[0] + r[2], m[0] + m[2], r[1] + r[3], m[1] + m[3]
        gr, gi, hr, hi = r[0] - r[2], m[0] - m[2], r[1] - r[3], m[1] - m[3]
        folded = (
            (er + fr, ei + fi),
            (gr + hi, gi - hr),
            (er - fr, ei - fi),
            (gr - hi, gi + hr),
        )
        if time == T - 1:
            ahead.wait()
        for q in range(RADIX):
            upper, lower = halves(jnp.concatenate(folded[q], axis=0))
            first = dot(jnp.concatenate([upper, lower], axis=0), table[q, 0])
            wave = first[: 2 * n] + first[2 * n :] + dot(upper, table[q, 1])
            now = jnp.concatenate(
                [wave[:n, :short] + wave[n:, short:], wave[n:, :short] - wave[:n, short:]],
                axis=1,
            )
            spectrum[time, q] = now
            if time:
                power = power_of(spectrum[time - 1, q] * now)
                if time > 1:
                    power = power + share[:, q]
                if time == T - 1:
                    beyond = power_of(now * following[q])
                    power = power + jnp.where(here < p.parts - 1, beyond, 0.0)
                share[:, q] = power
                if time == T - 1:
                    for hop in range(1, p.parts):
                        across(hop, q).start()
        if time == 0:
            ahead.start()

    for kind in range(T + 1):
        if kind == T or p.main:
            for step in range(1, N):
                for copy in start(kind, partner(me, step, N)):
                    copy.wait_send()
    summed = []
    for q in range(RADIX):
        value = share[here, q]
        for hop in range(1, p.parts):
            across(hop, q).wait()
            value = value + shared[hop - 1, q]
        summed.append(value)
    lane = iota((rows, 128), 1)
    for tile in range(F // 128):
        begin = tile * 128 // RADIX
        block = begin // 128 * 128
        index = lane // RADIX + (begin - block)
        value = None
        for q in range(RADIX):
            picked = jnp.take_along_axis(summed[q][:, block : block + 128], index, axis=1)
            value = picked if value is None else jnp.where(lax.rem(lane, RADIX) == q, picked, value)
        out[:, tile * 128 : (tile + 1) * 128] = value


def per_device(visibility_real, visibility_imag, weights, labels, owner_of):
    row_count, times, channels = visibility_real.shape
    owners, parts = lax.axis_size("bl"), lax.axis_size("tm")
    p = Plan(row_count, times, channels, owner_of.shape[0], owners, parts)
    short = channels // RADIX
    inside = pl.BlockSpec(memory_space=pltpu.VMEM)
    outside = pl.BlockSpec(memory_space=pltpu.HBM)
    some = lambda count: max(count, 8)
    main, tail = some(p.main), some(p.tail)
    rows = p.per_owner // parts
    return pl.pallas_call(
        functools.partial(program_kernel, p),
        out_shape=jax.ShapeDtypeStruct((rows, channels), F32),
        in_specs=[outside] * 5,
        out_specs=inside,
        scratch_shapes=[
            pltpu.VMEM((times, row_count), I32),
            pltpu.VMEM((row_count // 128, 128), I32),
            pltpu.VMEM((1, p.groups), I32),
            pltpu.VMEM((times // 2, 2, row_count, 2, channels), BF16),
            pltpu.VMEM((times // 2, 2, some(2 * p.mains), channels), F32),
            pltpu.VMEM((2, some(p.tails), channels), F32),
            pltpu.VMEM((times, owners, main, channels), I32),
            pltpu.VMEM((owners, tail, channels), I32),
            pltpu.VMEM((owners, 1, 128), F32),
            pltpu.VMEM((times, owners, 1, 128), F32),
            pltpu.VMEM((times, owners, main, channels), I32),
            pltpu.VMEM((owners, tail, channels), I32),
            pltpu.VMEM((owners, 1, 128), F32),
            pltpu.VMEM((times, owners, 1, 128), F32),
            pltpu.VMEM((RADIX, 2, short, 2 * short), BF16),
            pltpu.VMEM((1, channels), F32),
            pltpu.VMEM((2, times * p.per_owner, channels), F32),
            pltpu.VMEM((2, some(2 * p.mains), channels), BF16),
            pltpu.VMEM((times, RADIX, p.per_owner, 2 * short), F32),
            pltpu.VMEM((RADIX, p.per_owner, 2 * short), F32),
            pltpu.VMEM((parts, RADIX, rows, short), F32),
            pltpu.VMEM((parts - 1, RADIX, rows, short), F32),
            pltpu.SemaphoreType.DMA((times // 2, 2)),
            pltpu.SemaphoreType.DMA((3,)),
            pltpu.SemaphoreType.DMA((2 * times + 2, owners)),
            pltpu.SemaphoreType.DMA((2 * times + 2, owners)),
            pltpu.SemaphoreType.DMA((2,)),
            pltpu.SemaphoreType.DMA((parts - 1, RADIX)),
            pltpu.SemaphoreType.DMA((parts - 1, RADIX)),
        ],
        compiler_params=pltpu.CompilerParams(
            collective_id=0, has_side_effects=True, vmem_limit_bytes=60 * 2**20
        ),
    )(visibility_real, visibility_imag, weights.T, labels.reshape(-1, 128), owner_of[None, :])


def solution(mesh):
    placed = (P("bl", "tm", None), P("bl", "tm", None), P("bl", "tm"), P("bl"), P())
    return jax.shard_map(
        per_device, mesh=mesh, in_specs=placed, out_specs=P(("bl", "tm"), None), check_vma=False
    )
```

time: 70.5 us -> 69.2 us (0.982)
  local copies, waits for them, and re-layouts: 2.72 us -> 1.47 us
    broadcast_in_dim x1 -> x0, local copies, waits for them, and re-layouts: 1.24 us -> none  [per_device(): labels[None, :]]
where the time goes in v2:
time: 69.2 us; the launch traced here: 68.7 us
  Pallas kernels  67.2 us (97%)
  local copies, waits for them, and re-layouts  1.47 us (2%)
    pallas_call x1, Pallas kernels, per_device(): pl.pallas_call(functools.partial(program_kernel, p), out_shape=jax.ShapeD...  67.2 us
    unnamed x1, local copies, waits for them, and re-layouts  1.47 us

profile of v2, /device:TPU:9, one launch (start us, length us, event | category | flops | bytes accessed | tf_op | source)
XLA Modules:
  0.0 68.7 jit_solution(15137753414539710755)
XLA Ops:
  0.0 67.2 %shard_map.55 = f32[16,1024]{1,0:T(8,128)} custom-call(bf16[384,4,1024]{2,1,0:T(4,128)(2,1)} %vis_real.1, bf16[384,4,1024]{2,1,0:T(4,128)(2,1)} %vis_imag.1, s32[4,384]{1,0:T(4,128)} %bitcast.3, s32[3,128]{1,0:T(4,128)} %bitcast.4, s32[1,512]{1,0:T(1,128)} %bitcast.5), custom_call_target="tpu_custom_call" | custom-call | tf_op jit(solution)/shard_map/pallas_call | solution.py:514
  67.3 1.5 %copy.7 = f32[16,1024]{1,0:T(8,128)} copy(f32[16,1024]{1,0:T(8,128)} %shard_map.55) | data formatting | bytes 131072

commit v3 on v2

--- a/solution.py
+++ b/solution.py
@@ -53,14 +53,14 @@
         self.tail = -(-self.extra * times // 8) * 8
         self.mains = owners * self.main
         self.tails = owners * self.tail
-        assert times * self.main + 2 * self.tail <= 128
+        assert times * self.main + self.tail <= 128
 
 
 def program_kernel(
     plan, vis_real, vis_imag, weights, labels, owner_of, out,
     weight_in, label_in, owner_in,
-    fresh, part, part_tail, send, send_tail, send_note, send_step,
-    came, came_tail, came_note, came_step,
+    fresh, part, part_tail, send, send_tail, send_note,
+    came, came_tail, came_note,
     table, taper, total, planes, spectrum, following, share, shared,
     loads, small, sends, arrivals, ahead_sems, tail_sends, tail_arrivals,
 ):
@@ -86,8 +86,9 @@
             copy = pltpu.make_async_copy(
                 source.at[:, pl.ds(2 * pair, 2)], fresh.at[pair, which], loads.at[pair, which]
             )
-            copy.start()
             incoming.append(copy)
+    for copy in incoming[:2]:
+        copy.start()
 
     barrier = pltpu.get_barrier_semaphore()
     for hop in range(1, N):
@@ -162,15 +163,15 @@
 
     base_tail = T * p.main
     note = jnp.zeros((N, 1, 128), F32)
+    send_note[...] = jnp.zeros_like(send_note)
 
     def start(kind, peer):
         if kind < T:
             pieces = [(send.at[kind], came.at[kind], kind)]
-            pieces.append((send_step.at[kind], came_step.at[kind], T + kind))
         else:
-            pieces = [(send_note, came_note, 2 * T + 1)]
+            pieces = [(send_note, came_note, T + 1)]
             if p.extra:
-                pieces.append((send_tail, came_tail, 2 * T))
+                pieces.append((send_tail, came_tail, T))
         return [
             pltpu.make_async_remote_copy(
                 src_ref=source.at[peer],
@@ -186,11 +187,10 @@
     def arrive(kind, source):
         if kind < T:
             pieces = [(send.at[kind], came.at[kind], kind)]
-            pieces.append((send_step.at[kind], came_step.at[kind], T + kind))
         else:
-            pieces = [(send_note, came_note, 2 * T + 1)]
+            pieces = [(send_note, came_note, T + 1)]
             if p.extra:
-                pieces.append((send_tail, came_tail, 2 * T))
+                pieces.append((send_tail, came_tail, T))
         return [
             pltpu.make_async_remote_copy(
                 src_ref=origin.at[source],
@@ -223,44 +223,38 @@
         at = pl.multiple_of(time % 2 * p.mains + o * p.main, 16)
         rows = pl.ds(at, p.main)
         code, step = encode(part[time // 2, 0, rows], part[time // 2, 1, rows])
-        return code, laid(step, p.main, 0)[0]
-
-    def handle_main(time):
+        send_note[o, 1:2] += laid(step, p.main, time * p.main)[0]
+        return code
+
+    def encode_tail(o):
+        rows = pl.ds(pl.multiple_of(o * p.tail, 8), p.tail)
+        code, step = encode(part_tail[0, rows], part_tail[1, rows])
+        send_note[o, 1:2] += laid(step, p.tail, base_tail)[0]
+        return code
+
+    def handle_main(time, now):
         def one(step, carry):
             peer = partner(me, step, N)
-            code, steps = encode_main(time, peer)
-            send[time, peer] = code
-            send_step[time, peer] = steps
-            post(time, peer)
+            send[time, peer] = encode_main(time, peer)
+            if now:
+                post(time, peer)
             return carry
 
-        lax.fori_loop(1, N, one, 0)
-        code, steps = encode_main(time, me)
-        came[time, me] = code
-        came_step[time, me] = steps
-
-    def encode_tail(o):
-        at = pl.multiple_of(o * p.tail, 8)
-        code, step = encode(part_tail[0, pl.ds(at, p.tail)], part_tail[1, pl.ds(at, p.tail)])
-        return code, send_note[o] + laid(step, p.tail, base_tail + p.tail)[0]
+        if now:
+            lax.fori_loop(N // 2, N, one, 0)
+            lax.fori_loop(1, N // 2, one, 0)
+        else:
+            lax.fori_loop(1, N, one, 0)
+        came[time, me] = encode_main(time, me)
 
     def handle_tail():
         def one(step, carry):
             peer = partner(me, step, N)
-            if p.extra:
-                code, facts = encode_tail(peer)
-                send_tail[peer] = code
-                send_note[peer] = facts
-            post(T, peer)
+            send_tail[peer] = encode_tail(peer)
             return carry
 
         lax.fori_loop(1, N, one, 0)
-        if p.extra:
-            code, facts = encode_tail(me)
-            came_tail[me] = code
-            came_note[me] = facts
-        else:
-            came_note[me] = send_note[me]
+        came_tail[me] = encode_tail(me)
 
     all_rows = 2 * p.mains + p.tails
     tail_weight = jnp.zeros((p.tails, 1), F32)
@@ -282,35 +276,43 @@
         folder = folder.astype(BF16)
         for copy in incoming[2 * pair : 2 * pair + 2]:
             copy.wait()
-        for which in range(2):
-            made = dot(folder, fresh[pair, which].reshape(both, F))
-            if p.main:
-                part[pair, which] = made[: 2 * p.mains]
-            if p.extra:
-                if pair:
-                    part_tail[which] += made[2 * p.mains :]
-                else:
-                    part_tail[which] = made[2 * p.mains :]
+        for copy in incoming[2 * pair + 2 : 2 * pair + 4]:
+            copy.start()
+        bounds = [0, all_rows]
+        if pair == 0 and p.main:
+            bounds = [0, p.mains, all_rows]
+        for low, high in zip(bounds, bounds[1:]):
+            for which in range(2):
+                made = dot(folder[low:high], fresh[pair, which].reshape(both, F))
+                middle = max(2 * p.mains - low, 0)
+                if middle:
+                    part[pair, which, low : min(high, 2 * p.mains)] = made[:middle]
+                if p.extra and high == all_rows:
+                    if pair:
+                        part_tail[which] += made[middle:]
+                    else:
+                        part_tail[which] = made[middle:]
+            if pair == 0 and low == 0:
+                pl.semaphore_wait(barrier, N + p.parts - 2)
+                if p.main:
+                    handle_main(0, True)
         if p.main:
             for which in range(2):
                 fact = sums[which * p.mains : (which + 1) * p.mains] * n + rank_main
                 note = note + laid(fact, p.main, (2 * pair + which) * p.main)
         if p.extra:
             tail_weight = tail_weight + sums[2 * p.mains :]
-        if pair == 0:
-            pl.semaphore_wait(barrier, N + p.parts - 2)
-            if p.main:
-                handle_main(0)
-        if pair == pairs - 1:
-            if p.extra:
-                note = note + laid(tail_weight * n + rank_tail, p.tail, base_tail)
-            send_note[...] = note
-            handle_tail()
-            if p.main:
-                handle_main(1)
-        if p.main and pair:
-            handle_main(2 * pair)
-            handle_main(2 * pair + 1)
+        if p.main:
+            for time in range(max(2 * pair, 1), 2 * pair + 2):
+                handle_main(time, False)
+    if p.extra:
+        note = note + laid(tail_weight * n + rank_tail, p.tail, base_tail)
+        handle_tail()
+    send_note[:, 0:1] = note
+    came_note[me] = send_note[me]
+    for kind in [T] + list(range(1, T if p.main else 1)):
+        for step in range(1, N):
+            post(kind, partner(me, step, N))
 
     turn = 2.0 * math.pi / F
     phase = turn * iota((1, F), 1).astype(F32)
@@ -342,6 +344,10 @@
         for copy in arrive(kind, source):
             copy.wait_recv()
 
+    cut = 1 if N & (N - 1) else 2
+    group = N // cut
+    mine = me // group
+
     def split(code):
         imag = (code << 16) >> 16
         parts = (code >> 24, (code >> 16) & 255, imag >> 8, imag & 255)
@@ -363,15 +369,20 @@
 
     for step in range(1, N):
         wait_for(T, partner(me, step, N))
-    notes = came_note[...]
+    facts, steps = came_note[:, 0], came_note[:, 1]
     rank_row = iota((n, 1), 0)
-    main_facts = []
+    main_picks = []
     if p.main:
-        main_facts = [facts_of(notes, p.main, time * p.main) for time in range(T)]
+        for time in range(T):
+            rank, heft = facts_of(facts, p.main, time * p.main)
+            chosen = rank_row == rank
+            heft = jnp.sum(jnp.where(chosen, heft, 0.0), axis=1, keepdims=True)
+            selector = jnp.where(chosen, gathered(steps, p.main, time * p.main), 0.0)
+            main_picks.append((selector, heft))
     tail_sums = []
     if p.extra:
-        tail_rank, tail_heft = facts_of(notes, p.tail, base_tail)
-        tail_step = gathered(notes, p.tail, base_tail + p.tail)
+        tail_rank, tail_heft = facts_of(facts, p.tail, base_tail)
+        tail_step = gathered(steps, p.tail, base_tail)
         pieces = split(came_tail[...].reshape(p.tails, F))
         lane = lax.rem(iota((1, p.tails), 1), p.tail)
         lane_time = jnp.where(lane < p.extra * T, lane // p.extra, T)
@@ -414,29 +425,33 @@
             weight_sum = weight_sum + tail_sums[time]
         if p.main:
 
-            def unpack(source):
-                for which, piece in enumerate(split(came[time, source])):
-                    at = which % 2 * p.mains + source * p.main
-                    planes[which // 2, pl.ds(pl.multiple_of(at, 16), p.main)] = piece
-
-            def one(step, carry):
-                source = partner(me, step, N)
-                wait_for(time, source)
-                unpack(source)
-                return carry
-
-            unpack(me)
-            lax.fori_loop(1, N, one, 0)
-            rank, heft = main_facts[time]
-            chosen = rank_row == rank
-            selector = jnp.where(chosen, gathered(came_step[time], p.main, 0), 0.0)
-            selector = jnp.concatenate([256.0 * selector, selector], axis=1).astype(BF16)
-            weight_sum = weight_sum + jnp.sum(jnp.where(chosen, heft, 0.0), axis=1, keepdims=True)
-            real, imag = dot(selector, planes[0]), dot(selector, planes[1])
-        block = pl.ds(time * n, n)
-        if p.main and p.extra:
-            real, imag = real + total[0, block], imag + total[1, block]
-        elif p.extra:
+            selector_all, heft = main_picks[time]
+            weight_sum = weight_sum + heft
+            real = imag = 0.0
+            if p.extra:
+                block = pl.ds(time * n, n)
+                real, imag = total[0, block], total[1, block]
+            wide = group * p.main
+            for near in range(cut):
+                members = range(near * group, (near + 1) * group)
+                for step in members:
+                    source = partner(me, step, N) if step else me
+                    if step:
+                        wait_for(time, source)
+                    for which, piece in enumerate(split(came[time, source])):
+                        at = which % 2 * wide + lax.rem(source, group) * p.main
+                        at = pl.ds(pl.multiple_of(at, 16), p.main)
+                        planes[near, which // 2, at] = piece
+                selector = selector_all
+                if cut == 2:
+                    selector = jnp.where(
+                        (mine + near) % 2 == 0, selector[:, :wide], selector[:, wide:]
+                    )
+                selector = jnp.concatenate([256.0 * selector, selector], axis=1).astype(BF16)
+                real = real + dot(selector, planes[near, 0])
+                imag = imag + dot(selector, planes[near, 1])
+        else:
+            block = pl.ds(time * n, n)
             real, imag = total[0, block], total[1, block]
         scale = 1.0 / jnp.maximum(weight_sum, 1.0)
         window = taper[...]
@@ -471,9 +486,10 @@
                     beyond = power_of(now * following[q])
                     power = power + jnp.where(here < p.parts - 1, beyond, 0.0)
                 share[:, q] = power
-                if time == T - 1:
-                    for hop in range(1, p.parts):
-                        across(hop, q).start()
+                if time == T - 1 and q % 2 == 1:
+                    for part_q in range(q - 1, q + 1):
+                        for hop in range(1, p.parts):
+                            across(hop, part_q).start()
         if time == 0:
             ahead.start()
 
@@ -511,9 +527,10 @@
     some = lambda count: max(count, 8)
     main, tail = some(p.main), some(p.tail)
     rows = p.per_owner // parts
+    cut = 1 if owners & (owners - 1) else 2
     return pl.pallas_call(
         functools.partial(program_kernel, p),
-        out_shape=jax.ShapeDtypeStruct((rows, channels), F32),
+        out_shape=pltpu.VMEM((rows, channels), F32),
         in_specs=[outside] * 5,
         out_specs=inside,
         scratch_shapes=[
@@ -525,24 +542,22 @@
             pltpu.VMEM((2, some(p.tails), channels), F32),
             pltpu.VMEM((times, owners, main, channels), I32),
             pltpu.VMEM((owners, tail, channels), I32),
-            pltpu.VMEM((owners, 1, 128), F32),
-            pltpu.VMEM((times, owners, 1, 128), F32),
+            pltpu.VMEM((owners, 2, 128), F32),
             pltpu.VMEM((times, owners, main, channels), I32),
             pltpu.VMEM((owners, tail, channels), I32),
-            pltpu.VMEM((owners, 1, 128), F32),
-            pltpu.VMEM((times, owners, 1, 128), F32),
+            pltpu.VMEM((owners, 2, 128), F32),
             pltpu.VMEM((RADIX, 2, short, 2 * short), BF16),
             pltpu.VMEM((1, channels), F32),
             pltpu.VMEM((2, times * p.per_owner, channels), F32),
-            pltpu.VMEM((2, some(2 * p.mains), channels), BF16),
+            pltpu.VMEM((cut, 2, some(2 * p.mains) // cut, channels), BF16),
             pltpu.VMEM((times, RADIX, p.per_owner, 2 * short), F32),
             pltpu.VMEM((RADIX, p.per_owner, 2 * short), F32),
             pltpu.VMEM((parts, RADIX, rows, short), F32),
             pltpu.VMEM((parts - 1, RADIX, rows, short), F32),
             pltpu.SemaphoreType.DMA((times // 2, 2)),
             pltpu.SemaphoreType.DMA((3,)),
-            pltpu.SemaphoreType.DMA((2 * times + 2, owners)),
-            pltpu.SemaphoreType.DMA((2 * times + 2, owners)),
+            pltpu.SemaphoreType.DMA((times + 2, owners)),
+            pltpu.SemaphoreType.DMA((times + 2, owners)),
             pltpu.SemaphoreType.DMA((2,)),
             pltpu.SemaphoreType.DMA((parts - 1, RADIX)),
             pltpu.SemaphoreType.DMA((parts - 1, RADIX)),

time: 69.2 us -> 64.8 us (0.936)
  Pallas kernels: 67.2 us -> 63.7 us
  local copies, waits for them, and re-layouts: 1.47 us -> 0.63 us
    pallas_call x1, Pallas kernels: 67.2 us -> 63.7 us  [per_device(): pl.pallas_call(functools.partial(program_kernel, p), out_shape=pltpu.VMEM...]
    unnamed x1, local copies, waits for them, and re-layouts: 1.47 us -> 0.63 us
where the time goes in v3:
time: 64.8 us; the launch traced here: 64.3 us
  Pallas kernels  63.7 us (98%)
    pallas_call x1, Pallas kernels, per_device(): pl.pallas_call(functools.partial(program_kernel, p), out_shape=pltpu.VMEM...  63.7 us

profile of v3, /device:TPU:9, one launch (start us, length us, event | category | flops | bytes accessed | tf_op | source)
XLA Modules:
  0.0 64.3 jit_solution(9702430632609991971)
XLA Ops:
  0.0 63.7 %shard_map.55 = f32[16,1024]{1,0:T(8,128)S(1)} custom-call(bf16[384,4,1024]{2,1,0:T(4,128)(2,1)} %vis_real.1, bf16[384,4,1024]{2,1,0:T(4,128)(2,1)} %vis_imag.1, s32[4,384]{1,0:T(4,128)} %bitcast.3, s32[3,128]{1,0:T(4,128)} %bitcast.4, s32[1,512]{1,0:T(1,128)} %bitcast.5), custom_call_target="tpu_custom_call" | custom-call | tf_op jit(solution)/shard_map/pallas_call | solution.py:531
  63.7 0.6 copy.7

commit v4 on v3

--- a/solution.py
+++ b/solution.py
@@ -107,20 +107,9 @@
     label = jnp.concatenate(
         [label_in[i : i + 1] for i in range(label_in.shape[0])], axis=1
     )
-    base = jnp.concatenate(
-        [
-            (label // 256).astype(F32),
-            lax.rem(label, 256).astype(F32),
-            weight_in[...].astype(F32),
-            jnp.zeros((-(T + 2) % 8, R), F32),
-        ],
-        axis=0,
-    )
-    doubled = dot(base.astype(BF16), spread)
-    label_twice = (doubled[0:1] * 256.0 + doubled[1:2]).astype(I32)
-    hit = (iota((G, both), 0) == label_twice).astype(F32).astype(BF16)
+    hit = (iota((G, R), 0) == label).astype(F32).astype(BF16)
     count = lax.dot_general(
-        jnp.ones((8, both), BF16), hit, (((1,), (1,)), ((), ())), preferred_element_type=F32
+        jnp.ones((8, R), BF16), hit, (((1,), (1,)), ((), ())), preferred_element_type=F32
     )
     present = (count[0:1] > 0.5).astype(F32)
     owner = owner_in[...]
@@ -129,31 +118,37 @@
     rank = jnp.sum(owned * earlier[:N], axis=0, keepdims=True)
     order = jnp.sum(owned * earlier[N:], axis=0, keepdims=True)
     info = jnp.concatenate([owner.astype(F32), order, jnp.zeros((6, G), F32)], axis=0)
-    placed = dot(info.astype(BF16), hit)
-    row_owner = placed[0:1].astype(I32)
-    row_order = placed[1:2].astype(I32)
+    placed = dot(info.astype(BF16), hit)[:2]
+    base = jnp.concatenate(
+        [placed, weight_in[...].astype(F32), jnp.zeros((-(T + 2) % 8, R), F32)], axis=0
+    )
+    doubled = dot(base.astype(BF16), spread)
+    row_owner = doubled[0:1].astype(I32)
+    row_order = doubled[1:2].astype(I32)
     second = lax.rem(iota((1, both), 1), 2)
 
-    listed = order.astype(I32)
-    seen = present > 0.5
-    rank_main = rank_tail = None
-    if p.main:
-        slot_main = jnp.where(seen & (listed < p.main), owner * p.main + listed, -1)
-        rank_main = jnp.sum(
-            jnp.where(iota((p.mains, G), 0) == slot_main, rank, 0.0), axis=1, keepdims=True
-        )
-    if p.extra:
-        slot_tail = jnp.where(
-            seen & (listed >= p.main), owner * p.extra + listed - p.main, -1
-        )
-        row = iota((p.tails, 1), 0)
-        within = lax.rem(row, p.tail)
-        slot_of_row = row // p.tail * p.extra + lax.rem(within, p.extra)
-        rank_tail = jnp.sum(
-            jnp.where((slot_of_row == slot_tail) & (within < p.extra * T), rank, 0.0),
-            axis=1,
-            keepdims=True,
-        )
+    def ranks():
+        listed = order.astype(I32)
+        seen = present > 0.5
+        rank_main = rank_tail = None
+        if p.main:
+            slot_main = jnp.where(seen & (listed < p.main), owner * p.main + listed, -1)
+            rank_main = jnp.sum(
+                jnp.where(iota((p.mains, G), 0) == slot_main, rank, 0.0), axis=1, keepdims=True
+            )
+        if p.extra:
+            slot_tail = jnp.where(
+                seen & (listed >= p.main), owner * p.extra + listed - p.main, -1
+            )
+            row = iota((p.tails, 1), 0)
+            within = lax.rem(row, p.tail)
+            slot_of_row = row // p.tail * p.extra + lax.rem(within, p.extra)
+            rank_tail = jnp.sum(
+                jnp.where((slot_of_row == slot_tail) & (within < p.extra * T), rank, 0.0),
+                axis=1,
+                keepdims=True,
+            )
+        return rank_main, rank_tail
 
     def laid(column, height, offset):
         shape = (column.shape[0], 128)
@@ -241,7 +236,7 @@
             return carry
 
         if now:
-            lax.fori_loop(N // 2, N, one, 0)
+            lax.fori_loop(N // 2, N, lambda i, c: one(N + N // 2 - 1 - i, c), 0)
             lax.fori_loop(1, N // 2, one, 0)
         else:
             lax.fori_loop(1, N, one, 0)
@@ -272,8 +267,7 @@
             - p.main,
         )
         folder = jnp.where(iota((all_rows, both), 0) == target, weight, 0.0)
-        sums = jnp.sum(folder, axis=1, keepdims=True)
-        folder = folder.astype(BF16)
+        full, folder = folder, folder.astype(BF16)
         for copy in incoming[2 * pair : 2 * pair + 2]:
             copy.wait()
         for copy in incoming[2 * pair + 2 : 2 * pair + 4]:
@@ -296,6 +290,9 @@
                 pl.semaphore_wait(barrier, N + p.parts - 2)
                 if p.main:
                     handle_main(0, True)
+        sums = jnp.sum(full, axis=1, keepdims=True)
+        if pair == 0:
+            rank_main, rank_tail = ranks()
         if p.main:
             for which in range(2):
                 fact = sums[which * p.mains : (which + 1) * p.mains] * n + rank_main

time: 64.8 us -> 64.5 us (level)
  no operation moved by 1% of the time
where the time goes in v4:
time: 64.5 us; the launch traced here: 64 us
  Pallas kernels  63.4 us (98%)
    pallas_call x1, Pallas kernels, per_device(): pl.pallas_call(functools.partial(program_kernel, p), out_shape=pltpu.VMEM...  63.4 us

profile of v4, /device:TPU:9, one launch (start us, length us, event | category | flops | bytes accessed | tf_op | source)
XLA Modules:
  0.0 64.0 jit_solution(11192985028543075373)
XLA Ops:
  0.0 63.4 %shard_map.55 = f32[16,1024]{1,0:T(8,128)S(1)} custom-call(bf16[384,4,1024]{2,1,0:T(4,128)(2,1)} %vis_real.1, bf16[384,4,1024]{2,1,0:T(4,128)(2,1)} %vis_imag.1, s32[4,384]{1,0:T(4,128)} %bitcast.3, s32[3,128]{1,0:T(4,128)} %bitcast.4, s32[1,512]{1,0:T(1,128)} %bitcast.5), custom_call_target="tpu_custom_call" | custom-call | tf_op jit(solution)/shard_map/pallas_call | solution.py:528
  63.4 0.6 copy.7
